TPU v7x, 32 devices: a whole 2x2x4 slice. The times are simulated.
32 devices in a mesh: dp: 2 (over x), row: 4 (over z), col: 4 (over y, core).
Axes of the slice: x: 2, y: 2, z: 4, core: 2. Of those that a mesh axis runs over, the one named last changes fastest.
Arguments:
- expand_gradient: bfloat16 [2, 4096, 5120], P('dp', 'row', 'col'), may hold values from -24 to 24, as said below
- expand_master: float32 [4096, 5120], P(('row', 'dp'), 'col'), may hold values from -0.12 to 0.12
- expand_rows: float32 [4096], P(('row', 'dp')), may hold values from 0.01 to 1
- expand_columns: float32 [5120], P('col'), may hold values from 0.01 to 1
- contract_gradient: bfloat16 [2, 5120, 4096], P('dp', 'row', 'col'), may hold values from -24 to 24, as said below
- contract_master: float32 [5120, 4096], P(('row', 'dp'), 'col'), may hold values from -0.12 to 0.12
- contract_rows: float32 [5120], P(('row', 'dp')), may hold values from 0.01 to 1
- contract_columns: float32 [4096], P('col'), may hold values from 0.01 to 1
- attend_gradient: bfloat16 [2, 4096, 4096], P('dp', 'row', 'col'), may hold values from -24 to 24, as said below
- attend_master: float32 [4096, 4096], P(('row', 'dp'), 'col'), may hold values from -0.12 to 0.12
- attend_rows: float32 [4096], P(('row', 'dp')), may hold values from 0.01 to 1
- attend_columns: float32 [4096], P('col'), may hold values from 0.01 to 1
Outputs:
- expand_updated: float32 [4096, 5120], P(('row', 'dp'), 'col')
- expand_weights: bfloat16 [4096, 5120], P('row', 'col')
- expand_rows_next: float32 [4096], P(('row', 'dp'))
- expand_columns_next: float32 [5120], P('col')
- expand_step: float32 [4096, 5120], P(('row', 'dp'), 'col')
- contract_updated: float32 [5120, 4096], P(('row', 'dp'), 'col')
- contract_weights: bfloat16 [5120, 4096], P('row', 'col')
- contract_rows_next: float32 [5120], P(('row', 'dp'))
- contract_columns_next: float32 [4096], P('col')
- contract_step: float32 [5120, 4096], P(('row', 'dp'), 'col')
- attend_updated: float32 [4096, 4096], P(('row', 'dp'), 'col')
- attend_weights: bfloat16 [4096, 4096], P('row', 'col')
- attend_rows_next: float32 [4096], P(('row', 'dp'))
- attend_columns_next: float32 [4096], P('col')
- attend_step: float32 [4096, 4096], P(('row', 'dp'), 'col')
Inputs may be any that keep to these rules, and one draw needn't show every extreme that they name: `expand_gradient`: each replica's gradient, of any scale from entry to entry. `contract_gradient`: each replica's gradient, of any scale from entry to entry. `attend_gradient`: each replica's gradient, of any scale from entry to entry.
All inputs are finite; a program needn't handle non-finite values.
Results may differ from a plain program's by a relative error of at most 0.0004.
Values may be sent and summed in bfloat16 or wider, within the bound.
A program may use at most 128 MiB of HBM per device.

v0:
```python
import jax
import jax.numpy as jnp
from jax import lax
from jax.sharding import PartitionSpec as P

tiny_square = 1e-30
decay_rate = 0.9
learn_rate = 0.01


def finish(update_raw, clip_total, master, full_size):
    clip_scale = jnp.maximum(1.0, jnp.sqrt(clip_total / full_size))
    step_taken = update_raw / clip_scale
    updated = master - learn_rate * step_taken
    weights = lax.all_gather(updated.astype(jnp.bfloat16), "dp", axis=0, tiled=True)
    return (updated, weights, step_taken)


def reduce_gradient(gradient, dp_count):
    received = lax.all_to_all(gradient, "dp", split_axis=1, concat_axis=0, tiled=True)
    summed = jnp.sum(received.astype(jnp.float32), axis=0)
    return summed / dp_count


def body(
    expand_gradient,
    expand_master,
    expand_rows,
    expand_columns,
    contract_gradient,
    contract_master,
    contract_rows,
    contract_columns,
    attend_gradient,
    attend_master,
    attend_rows,
    attend_columns,
):
    groups = (
        (expand_gradient, expand_master, expand_rows, expand_columns),
        (contract_gradient, contract_master, contract_rows, contract_columns),
        (attend_gradient, attend_master, attend_rows, attend_columns),
    )
    dp_count = lax.axis_size("dp")
    col_count = lax.axis_size("col")
    split_count = dp_count * lax.axis_size("row")
    means = []
    for gradient, master, row_stat, column_stat in groups:
        means.append(reduce_gradient(gradient, dp_count))
    squares = [mean_grad * mean_grad + tiny_square for mean_grad in means]
    row_parts = [jnp.sum(square_block, axis=1) for square_block in squares]
    column_parts = [jnp.sum(square_block, axis=0) for square_block in squares]
    heights = [mean_grad.shape[0] * split_count for mean_grad in means]
    widths = [mean_grad.shape[1] * col_count for mean_grad in means]
    outputs = []
    for which in range(3):
        row_total = lax.psum(row_parts[which], "col")
        rows_next = decay_rate * groups[which][2] + (1.0 - decay_rate) * row_total / widths[which]
        column_total, rows_sum = lax.psum((column_parts[which], jnp.sum(rows_next)), ("dp", "row"))
        columns_next = (
            decay_rate * groups[which][3] + (1.0 - decay_rate) * column_total / heights[which]
        )
        row_mean = rows_sum / heights[which]
        update_raw = means[which] * jnp.sqrt(
            row_mean / (rows_next[:, None] * columns_next[None, :])
        )
        clip_total = lax.psum(jnp.sum(update_raw * update_raw), ("dp", "row", "col"))
        updated, weights, step_taken = finish(
            update_raw, clip_total, groups[which][1], heights[which] * widths[which]
        )
        outputs.extend([updated, weights, rows_next, columns_next, step_taken])
    return tuple(outputs)


def solution(mesh):
    return jax.shard_map(
        body,
        mesh=mesh,
        in_specs=(
            P("dp", "row", "col"),
            P(("row", "dp"), "col"),
            P(("row", "dp")),
            P("col"),
            P("dp", "row", "col"),
            P(("row", "dp"), "col"),
            P(("row", "dp")),
            P("col"),
            P("dp", "row", "col"),
            P(("row", "dp"), "col"),
            P(("row", "dp")),
            P("col"),
        ),
        out_specs=(
            P(("row", "dp"), "col"),
            P("row", "col"),
            P(("row", "dp")),
            P("col"),
            P(("row", "dp"), "col"),
            P(("row", "dp"), "col"),
            P("row", "col"),
            P(("row", "dp")),
            P("col"),
            P(("row", "dp"), "col"),
            P(("row", "dp"), "col"),
            P("row", "col"),
            P(("row", "dp")),
            P("col"),
            P(("row", "dp"), "col"),
        ),
        check_vma=False,
    )
```

profile of v0, /device:TPU:0, one launch (start us, length us, event | category | flops | bytes accessed | tf_op | source)
XLA Modules:
  0.0 387.2 jit_solution(6910142270513207531)
XLA Ops:
  7.2 6.8 %copy.41 = bf16[1,1024,1024]{2,0,1:T(2,128)(2,1)} copy(bf16[1,1024,1024]{2,1,0:T(8,128)(2,1)} %param.20) | data formatting | bytes 4194304 | tf_op args[8]
  13.9 0.5 broadcast.37
  14.4 12.8 %reduce.2 = bf16[1024,1024]{1,0:T(8,128)(2,1)S(1)} reduce(bf16[1024,1,1024]{2,1,0:T(2,128)(2,1)} %bitcast.22, bf16[]{:T(256)} %broadcast.37), dimensions={1}, to_apply=%bitcast.17.reduce_sub_computation | reduce | bytes 4194306
  27.2 2.5 reshape.58
  29.7 5.5 %all-to-all-start.2 = ((bf16[2,2,262144]{2,1,0:T(2,128)(2,1)}), bf16[2,2,262144]{2,1,0:T(2,128)(2,1)}, u32[]{:S(2)}, u32[]{:S(2)}) async-start(bf16[2,2,262144]{2,1,0:T(2,128)(2,1)} %reshape.58), calls=%async_computation.2 | async-start | bytes 4194304 | tf_op jit(solution)/shard_map/all_to_all | solution.py:20
  35.2 6.4 %copy.40 = bf16[1,1024,1280]{2,0,1:T(2,128)(2,1)} copy(bf16[1,1024,1280]{2,1,0:T(8,128)(2,1)S(1)} %copy-done.4) | data formatting | bytes 5242880 | tf_op args[0]
  41.6 26.6 %reduce = bf16[1024,1280]{1,0:T(8,128)(2,1)S(1)} reduce(bf16[1024,1,1280]{2,1,0:T(2,128)(2,1)} %bitcast.21, bf16[]{:T(256)} %broadcast.37), dimensions={1}, to_apply=%bitcast.16.reduce_sub_computation | reduce | bytes 5242882
  68.2 1.8 reshape.54
  70.0 5.8 %all-to-all-start = ((bf16[2,2,327680]{2,1,0:T(2,128)(2,1)}), bf16[2,2,327680]{2,1,0:T(2,128)(2,1)}, u32[]{:S(2)}, u32[]{:S(2)}) async-start(bf16[2,2,327680]{2,1,0:T(2,128)(2,1)} %reshape.54), calls=%async_computation | async-start | bytes 5242880 | tf_op jit(solution)/shard_map/all_to_all | solution.py:20
  75.9 18.2 %copy.39 = bf16[1,1280,1024]{2,0,1:T(2,128)(2,1)} copy(bf16[1,1280,1024]{2,1,0:T(8,128)(2,1)S(1)} %copy-done.5) | data formatting | bytes 5242880 | tf_op args[4]
  94.1 15.6 %reduce.1 = bf16[1280,1024]{1,0:T(8,128)(2,1)S(1)} reduce(bf16[1280,1,1024]{2,1,0:T(2,128)(2,1)} %bitcast.18, bf16[]{:T(256)} %broadcast.37), dimensions={1}, to_apply=%bitcast.15.reduce_sub_computation | reduce | bytes 5242882
  109.6 3.0 reshape.56
  112.6 4.1 %all-to-all-start.1 = ((bf16[2,2,327680]{2,1,0:T(2,128)(2,1)}), bf16[2,2,327680]{2,1,0:T(2,128)(2,1)S(1)}, u32[]{:S(2)}, u32[]{:S(2)}) async-start(bf16[2,2,327680]{2,1,0:T(2,128)(2,1)} %reshape.56), calls=%async_computation.1 | async-start | bytes 5242880 | tf_op jit(solution)/shard_map/all_to_all | solution.py:20
  116.8 0.2 all-gather.8.cloned.1.call-start
  116.9 4.3 %reshape.59 = bf16[1024,1,1024]{2,1,0:T(2,128)(2,1)} reshape(bf16[2,2,262144]{2,1,0:T(2,128)(2,1)} %all-to-all-done.2) | data formatting | bytes 4194304
  121.2 3.0 copy.35
  124.2 0.4 convert_reduce_fusion.2
  124.7 0.0 copy-start.1
  124.7 1.3 copy-done.1
  126.0 0.5 fusion.5
  126.5 5.1 %reshape.55 = bf16[1024,1,1280]{2,1,0:T(2,128)(2,1)} reshape(bf16[2,2,327680]{2,1,0:T(2,128)(2,1)} %all-to-all-done) | data formatting | bytes 5242880
  131.5 2.9 copy.31
  134.4 0.5 convert_reduce_fusion.1
  134.9 0.0 copy-start
  134.9 1.5 copy-done
  136.4 0.6 fusion.1
  137.0 11.3 %all-to-all-done.1 = bf16[2,2,327680]{2,1,0:T(2,128)(2,1)S(1)} async-done(((bf16[2,2,327680]{2,1,0:T(2,128)(2,1)}), bf16[2,2,327680]{2,1,0:T(2,128)(2,1)S(1)}, u32[]{:S(2)}, u32[]{:S(2)}) %all-to-all-start.1) | async-done | bytes 2621472 | tf_op jit(solution)/shard_map/all_to_all | solution.py:20
  148.3 3.7 reshape.57
  152.1 3.5 copy.33
  155.6 0.6 convert_reduce_fusion
  156.2 0.0 copy-start.14
  156.2 0.0 copy-start.17
  156.2 0.0 copy-start.18
  156.2 0.0 copy-start.13
  156.2 0.0 copy-start.15
  156.2 0.0 copy-start.16
  156.2 0.5 fusion.3
  156.8 6.2 %all-reduce.2 = (f32[512]{0:T(512)S(1)}, f32[640]{0:T(1024)S(1)}, f32[512]{0:T(512)S(1)}) all-reduce(f32[512]{0:T(512)S(1)} %get-tuple-element.17, f32[640]{0:T(1024)S(1)} %get-tuple-element.15, f32[512]{0:T(512)S(1)} %get-tuple-element.19), channel_id=1, replica_groups=mesh['dp'=2,'row'=4,'col'=4] {'col'}, use_global_device_ids=true, to_apply=%region_2.0 | all-reduce | flops 1664 | bytes 13312 | tf_op jit(solution)/shard_map/psum | solution.py:57
  163.0 0.6 fusion.10
  163.6 0.6 fusion.9
  164.2 38.0 %all-reduce.1 = (f32[1280]{0:T(1024)S(1)}, f32[]{:T(128)}, f32[1024]{0:T(1024)S(1)}, f32[]{:T(128)}, f32[1024]{0:T(1024)S(1)}, /*index=5*/f32[]{:T(128)}) all-reduce(f32[1280]{0:T(1024)S(1)} %get-tuple-element.18, f32[]{:T(128)} %get-tuple-element.48, ...), channel_id=1, replica_groups=mesh['dp'=2,'row'=4,'col'=4] {'dp','row'}, use_global_device_ids=true, to_apply=%region_6.0 | all-reduce | flops 3331 | bytes 26648 | tf_op jit(solution)/shard_map/psum | solution.py:59
  203.5 0.0 copy-start.7
  203.5 0.0 copy-start.10
  204.2 0.0 copy-start.8
  204.2 0.0 copy-start.2
  204.2 3.8 multiply_reduce_fusion.1
  208.0 2.3 multiply_reduce_fusion
  210.3 2.0 multiply_reduce_fusion.2
  212.2 37.2 %all-reduce = (f32[]{:T(128)}, f32[]{:T(128)}, f32[]{:T(128)}) all-reduce(f32[]{:T(128)} %multiply_reduce_fusion.1, f32[]{:T(128)} %multiply_reduce_fusion, f32[]{:T(128)} %multiply_reduce_fusion.2), channel_id=1, replica_groups=mesh['dp'=2,'row'=4,'col'=4] {'dp','row','col'}, use_global_device_ids=true, to_apply=%region_8.0 | all-reduce | flops 3 | bytes 24 | tf_op jit(solution)/shard_map/psum | solution.py:67
  250.2 5.9 %fusion.6 = (bf16[512,1024]{1,0:T(8,128)(2,1)}, f32[512,1024]{1,0:T(8,128)}, f32[512,1024]{1,0:T(8,128)}) fusion(f32[512,1024]{1,0:T(8,128)} %param.21, f32[]{:T(128)S(6)} %max.11, f32[1024]{0:T(1024)S(1)} %multiply_add_fusion.4, f32[512]{0:T(512)S(1)} %get-tuple-element.77, f32[]{:T(128)S(6)} %div.136, f32[512,1024]{1,0:T(8,128)} %copy-done.1), kind=kLoop, calls=%fused_computation.30 | loop fusion | flops 4194304 | bytes 9443336 | tf_op jit(solution)/shard_map/convert_element_type | solution.py:15
  256.1 0.0 all-gather.8.cloned.1.call-update
  256.1 0.0 all-gather.4.cloned.1.call-start
  256.9 6.7 %fusion.8 = (bf16[512,1280]{1,0:T(8,128)(2,1)}, f32[512,1280]{1,0:T(8,128)}, f32[512,1280]{1,0:T(8,128)}) fusion(f32[512,1280]{1,0:T(8,128)} %param.13, f32[]{:T(128)S(6)} %max.9, f32[1280]{0:T(1024)S(1)} %multiply_add_fusion.3, f32[512]{0:T(512)S(1)} %get-tuple-element.67, f32[]{:T(128)S(6)} %div.112, f32[512,1280]{1,0:T(8,128)} %copy-done), kind=kLoop, calls=%fused_computation.32 | loop fusion | flops 5242880 | bytes 11803656 | tf_op jit(solution)/shard_map/convert_element_type | solution.py:15
  263.5 0.0 all-gather.4.cloned.1.call-update
  263.5 0.0 all-gather.6.cloned.1.call-start
  264.3 6.3 %fusion.7 = (bf16[640,1024]{1,0:T(8,128)(2,1)}, f32[640,1024]{1,0:T(8,128)}, f32[640,1024]{1,0:T(8,128)}) fusion(f32[640,1024]{1,0:T(8,128)} %param.17, f32[]{:T(128)S(6)} %max.10, f32[1024]{0:T(1024)S(1)} %multiply_add_fusion.5, f32[640]{0:T(1024)S(1)} %get-tuple-element.72, f32[]{:T(128)S(6)} %div.124, f32[640,1024]{1,0:T(8,128)S(1)} %convert_reduce_fusion), kind=kLoop, calls=%fused_computation.31 | loop fusion | flops 5242880 | bytes 11803144 | tf_op jit(solution)/shard_map/convert_element_type | solution.py:15
  270.5 0.0 all-gather.6.cloned.1.call-update
  270.6 20.2 %all-gather.8.cloned.1.call-done = bf16[1024,1024]{1,0:T(8,128)(2,1)} async-done(((bf16[512,1024]{1,0:T(8,128)(2,1)}), bf16[1024,1024]{1,0:T(8,128)(2,1)}) %all-gather.8.cloned.1.call-update) | async-done | bytes 2097168 | tf_op jit(solution)/shard_map/all_gather | solution.py:15
  290.7 41.1 %all-gather.4.cloned.1.call-done = bf16[1024,1280]{1,0:T(8,128)(2,1)} async-done(((bf16[512,1280]{1,0:T(8,128)(2,1)}), bf16[1024,1280]{1,0:T(8,128)(2,1)}) %all-gather.4.cloned.1.call-update) | async-done | bytes 2621456 | tf_op jit(solution)/shard_map/all_gather | solution.py:15
  331.9 41.2 %all-gather.6.cloned.1.call-done = bf16[1280,1024]{1,0:T(8,128)(2,1)} async-done(((bf16[640,1024]{1,0:T(8,128)(2,1)}), bf16[1280,1024]{1,0:T(8,128)(2,1)}) %all-gather.6.cloned.1.call-update) | async-done | bytes 2621456 | tf_op jit(solution)/shard_map/all_gather | solution.py:15
  373.1 3.5 copy.45
  376.6 1.5 copy.46
  378.1 1.0 copy-done.6
  379.1 1.3 copy.47
  (28 shorter events, 0.1 us)
Async XLA Ops:
  29.7 5.5 %copy-start.4 = (bf16[1,1024,1280]{2,1,0:T(8,128)(2,1)S(1)}, bf16[1,1024,1280]{2,1,0:T(8,128)(2,1)}, u32[]{:S(2)}) copy-start(bf16[1,1024,1280]{2,1,0:T(8,128)(2,1)} %param.12) | copy-start | bytes 7864324
  29.7 40.3 %all-to-all-start.2 = ((bf16[2,2,262144]{2,1,0:T(2,128)(2,1)}), bf16[2,2,262144]{2,1,0:T(2,128)(2,1)}, u32[]{:S(2)}, u32[]{:S(2)}) async-start(bf16[2,2,262144]{2,1,0:T(2,128)(2,1)} %reshape.58), calls=%async_computation.2 | async-start | bytes 4194304 | tf_op jit(solution)/shard_map/all_to_all | solution.py:20
  70.0 5.8 %copy-start.5 = (bf16[1,1280,1024]{2,1,0:T(8,128)(2,1)S(1)}, bf16[1,1280,1024]{2,1,0:T(8,128)(2,1)}, u32[]{:S(2)}) copy-start(bf16[1,1280,1024]{2,1,0:T(8,128)(2,1)} %param.16) | copy-start | bytes 7864324
  70.0 42.6 %all-to-all-start = ((bf16[2,2,327680]{2,1,0:T(2,128)(2,1)}), bf16[2,2,327680]{2,1,0:T(2,128)(2,1)}, u32[]{:S(2)}, u32[]{:S(2)}) async-start(bf16[2,2,327680]{2,1,0:T(2,128)(2,1)} %reshape.54), calls=%async_computation | async-start | bytes 5242880 | tf_op jit(solution)/shard_map/all_to_all | solution.py:20
  112.6 35.7 %all-to-all-start.1 = ((bf16[2,2,327680]{2,1,0:T(2,128)(2,1)}), bf16[2,2,327680]{2,1,0:T(2,128)(2,1)S(1)}, u32[]{:S(2)}, u32[]{:S(2)}) async-start(bf16[2,2,327680]{2,1,0:T(2,128)(2,1)} %reshape.56), calls=%async_computation.1 | async-start | bytes 5242880 | tf_op jit(solution)/shard_map/all_to_all | solution.py:20
  116.8 174.0 %all-gather.8.cloned.1.call-start = ((), (), s32[]{:S(2)}) async-start(), calls=%async_computation.5 | async-start | bytes 3145728 | tf_op jit(solution)/shard_map/all_gather | solution.py:15
  124.7 1.3 copy-start.1
  134.9 1.5 copy-start
  156.2 6.8 %copy-start.14 = (f32[640]{0:T(1024)S(1)}, f32[640]{0:T(1024)}, u32[]{:S(2)}) copy-start(f32[640]{0:T(1024)} %param.18) | copy-start | bytes 7684
  156.2 7.4 %copy-start.17 = (f32[512]{0:T(512)S(1)}, f32[512]{0:T(512)}, u32[]{:S(2)}) copy-start(f32[512]{0:T(512)} %param.22) | copy-start | bytes 6148
  156.2 7.4 %copy-start.18 = (f32[512]{0:T(512)S(1)}, f32[512]{0:T(512)}, u32[]{:S(2)}) copy-start(f32[512]{0:T(512)} %param.14) | copy-start | bytes 6148
  156.2 47.3 %copy-start.13 = (f32[1280]{0:T(1024)S(1)}, f32[1280]{0:T(1024)}, u32[]{:S(2)}) copy-start(f32[1280]{0:T(1024)} %param.15) | copy-start | bytes 15364
  156.2 47.3 %copy-start.15 = (f32[1024]{0:T(1024)S(1)}, f32[1024]{0:T(1024)}, u32[]{:S(2)}) copy-start(f32[1024]{0:T(1024)} %param.19) | copy-start | bytes 12292
  156.2 48.0 %copy-start.16 = (f32[1024]{0:T(1024)S(1)}, f32[1024]{0:T(1024)}, u32[]{:S(2)}) copy-start(f32[1024]{0:T(1024)} %param.23) | copy-start | bytes 12292
  163.6 100.7 %copy-start.9 = (f32[640]{0:T(1024)}, f32[640]{0:T(1024)S(1)}, u32[]{:S(2)}) copy-start(f32[640]{0:T(1024)S(1)} %get-tuple-element.72) | copy-start | bytes 7684
  164.2 86.0 %copy-start.11 = (f32[512]{0:T(512)}, f32[512]{0:T(512)S(1)}, u32[]{:S(2)}) copy-start(f32[512]{0:T(512)S(1)} %get-tuple-element.77) | copy-start | bytes 6148
  164.2 92.6 %copy-start.12 = (f32[512]{0:T(512)}, f32[512]{0:T(512)S(1)}, u32[]{:S(2)}) copy-start(f32[512]{0:T(512)S(1)} %get-tuple-element.67) | copy-start | bytes 6148
  203.5 53.3 %copy-start.7 = (f32[1280]{0:T(1024)}, f32[1280]{0:T(1024)S(1)}, u32[]{:S(2)}) copy-start(f32[1280]{0:T(1024)S(1)} %multiply_add_fusion.3) | copy-start | bytes 15364
  203.5 60.7 %copy-start.10 = (f32[1024]{0:T(1024)}, f32[1024]{0:T(1024)S(1)}, u32[]{:S(2)}) copy-start(f32[1024]{0:T(1024)S(1)} %multiply_add_fusion.5) | copy-start | bytes 12292
  204.2 46.0 %copy-start.8 = (f32[1024]{0:T(1024)}, f32[1024]{0:T(1024)S(1)}, u32[]{:S(2)}) copy-start(f32[1024]{0:T(1024)S(1)} %multiply_add_fusion.4) | copy-start | bytes 12292
  204.2 6.1 %copy-start.2 = (f32[512,1024]{1,0:T(8,128)S(1)}, f32[512,1024]{1,0:T(8,128)}, u32[]{:S(2)}) copy-start(f32[512,1024]{1,0:T(8,128)} %copy-done.1) | copy-start | bytes 6291460
  256.1 75.8 %all-gather.4.cloned.1.call-start = ((), (), s32[]{:S(2)}) async-start(), calls=%async_computation.3 | async-start | bytes 3932160 | tf_op jit(solution)/shard_map/all_gather | solution.py:15
  263.5 109.5 %all-gather.6.cloned.1.call-start = ((), (), s32[]{:S(2)}) async-start(), calls=%async_computation.4 | async-start | bytes 3932160 | tf_op jit(solution)/shard_map/all_gather | solution.py:15
  373.1 3.6 copy-start.3
  376.6 2.5 copy-start.6
Sparse Core Ops, SparseCore 0:
  256.2 34.4 all-gather.7
  292.9 38.9 all-gather.3
  334.0 38.9 all-gather.5
where the time goes:
time: 393 us; the launch traced here: 387 us
  waiting for transfers between devices  114 us (29%)
  other arithmetic  86.1 us (22%)
  blocking collectives  81.4 us (21%)
  local copies, waits for them, and re-layouts  71.9 us (18%)
  between operations  18.3 us (5%)
  starting transfers between devices  15.7 us (4%)
    all_gather x3, waiting for transfers between devices, finish(): lax.all_gather(updated.astype(jnp.bfloat16), 'dp', axis=0, tiled=True)  102 us
    unnamed x51, local copies, waits for them, and re-layouts  62.5 us
    unnamed x3, other arithmetic  55 us
    psum x1, blocking collectives, body(): lax.psum((column_parts[which], jnp.sum(rows_next)), ('dp', 'row'))  38 us
    psum x1, blocking collectives, body(): lax.psum(jnp.sum(update_raw * update_raw), ('dp', 'row', 'col'))  37.2 us
    convert_element_type x3, other arithmetic, finish(): updated.astype(jnp.bfloat16)  18.8 us
    all_to_all x3, starting transfers between devices, reduce_gradient(): lax.all_to_all(gradient, 'dp', split_axis=1, concat_axis=0, tiled=True)  15.4 us
    all_to_all x3, waiting for transfers between devices, reduce_gradient(): lax.all_to_all(gradient, 'dp', split_axis=1, concat_axis=0, tiled=True)  11.3 us
  transfers between devices with their start and end apart: 6, of which 4 were waited for; matrix products, arithmetic and copies ran while one was open for 26% of the time, Pallas kernels for 0%

commit v1 on v0

v1 whole, which is shorter than its diff:
```python
import functools
import math

import jax
import jax.numpy as jnp
from jax import lax
from jax.experimental import pallas as pl
from jax.experimental.pallas import tpu as pltpu
from jax.sharding import PartitionSpec as P

tiny_square = 1e-30
decay_rate = 0.9
learn_rate = 0.01
LANES = 128
MESH = pl.DeviceIdType.MESH
f32 = jnp.float32
bf16 = jnp.bfloat16


def chunk_count(rows):
    return 2 if rows % 64 == 0 else 1


def block_rows(rows):
    return 32 if rows % 32 == 0 else rows


def kernel(axes, shapes, *refs):
    dp_count, row_count, col_count = axes
    refs = list(refs)

    def take(count):
        taken = refs[:count]
        del refs[:count]
        return taken

    grads, masters, row_stats, col_stats = take(3), take(3), take(3), take(3)
    out_updated, out_weights, out_rows, out_cols, out_step = (take(3) for _ in range(5))
    own, recv, field, hold, weights = (take(3) for _ in range(5))
    row_part, row_wide, col_acc = take(3), take(3), take(3)
    rows_buf, cols_row_buf, cols_dp_buf = take(3), take(3), take(3)
    sum_col_buf, sum_row_buf, sum_dp_buf = take(3), take(3), take(3)
    rs_sems, ag_sems, rows_sems, cr_sems, cd_sems, sc_sems, sr_sems, sd_sems = (
        take(2) for _ in range(8)
    )
    (local_sems,) = take(1)

    me = {name: lax.axis_index(name) for name in ("dp", "row", "col")}
    size = {"dp": dp_count, "row": row_count, "col": col_count}

    def peer(axis, offset):
        return lax.rem(me[axis] + offset, size[axis])

    local_in = []
    for k in range(3):
        a = pltpu.make_async_copy(grads[k].at[me["dp"]], own[k], local_sems.at[k])
        b = pltpu.make_async_copy(masters[k], hold[k], local_sems.at[3 + k])
        a.start()
        b.start()
        local_in.append((a, b))

    barrier = pltpu.get_barrier_semaphore()
    total_peers = 0
    for axis in ("dp", "row", "col"):
        for offset in range(1, size[axis]):
            pl.semaphore_signal(
                barrier, inc=1, device_id={axis: peer(axis, offset)}, device_id_type=MESH
            )
            total_peers += 1
    pl.semaphore_wait(barrier, total_peers)

    def rows_of(k, half):
        rows = shapes[k][0]
        count = chunk_count(rows)
        if half >= count:
            return None
        return pl.ds(half * (rows // count), rows // count)

    def scatter(k, half):
        part = rows_of(k, half)
        copies = []
        if part is not None:
            for offset in range(1, dp_count):
                other = peer("dp", offset)
                copies.append(
                    pltpu.make_async_remote_copy(
                        src_ref=grads[k].at[other, part],
                        dst_ref=recv[k].at[offset - 1, part],
                        send_sem=rs_sems[0].at[k, half, offset - 1],
                        recv_sem=rs_sems[1].at[k, half, offset - 1],
                        device_id={"dp": other},
                        device_id_type=MESH,
                    )
                )
        for copy in copies:
            copy.start()
        return copies

    def gather(k, half):
        part = rows_of(k, half)
        copies = []
        if part is not None:
            for offset in range(1, dp_count):
                copies.append(
                    pltpu.make_async_remote_copy(
                        src_ref=weights[k].at[part],
                        dst_ref=out_weights[k].at[me["dp"], part],
                        send_sem=ag_sems[0].at[k, half, offset - 1],
                        recv_sem=ag_sems[1].at[k, half, offset - 1],
                        device_id={"dp": peer("dp", offset)},
                        device_id_type=MESH,
                    )
                )
        for copy in copies:
            copy.start()
        return copies

    def share(axis, buf, sems, k):
        copies = []
        for offset in range(1, size[axis]):
            copies.append(
                pltpu.make_async_remote_copy(
                    src_ref=buf.at[me[axis]],
                    dst_ref=buf.at[me[axis]],
                    send_sem=sems[0].at[k, offset - 1],
                    recv_sem=sems[1].at[k, offset - 1],
                    device_id={axis: peer(axis, offset)},
                    device_id_type=MESH,
                )
            )
        for copy in copies:
            copy.start()
        return copies

    def finish(copies):
        for copy in copies:
            copy.wait()

    def total_of(buf, axis, part=slice(None)):
        result = buf[0, part]
        for which in range(1, size[axis]):
            result = result + buf[which, part]
        return result

    def fold(block):
        result = block[0:8]
        for start in range(8, block.shape[0], 8):
            result = result + block[start : start + 8]
        return result

    def mean_pass(k, half):
        rows, width = shapes[k]
        count = chunk_count(rows)
        if half >= count:
            return
        chunk = rows // count
        step = block_rows(chunk)
        tiles = width // LANES

        def body(i, carry):
            at = pl.ds(pl.multiple_of(half * chunk + i * step, step), step)
            along = jnp.zeros((step, LANES), f32)
            new = []
            for t in range(tiles):
                lanes = pl.ds(t * LANES, LANES)
                value = own[k][at, lanes].astype(f32)
                for offset in range(dp_count - 1):
                    value = value + recv[k][offset, at, lanes].astype(f32)
                value = value * (1.0 / dp_count)
                field[k][at, lanes] = value
                square = value * value + tiny_square
                along = along + square
                new.append(carry[t] + fold(square))
            row_part[k][at, :] = along
            return tuple(new)

        if half == 0:
            init = tuple(jnp.zeros((8, LANES), f32) for _ in range(tiles))
        else:
            init = tuple(col_acc[k][:, t * LANES : (t + 1) * LANES] for t in range(tiles))
        result = lax.fori_loop(0, chunk // step, body, init)
        for t in range(tiles):
            col_acc[k][:, t * LANES : (t + 1) * LANES] = result[t]

    def stats(k):
        rows, width = shapes[k]
        padded = row_part[k].shape[0]
        if padded != rows:
            row_part[k][rows:, :] = jnp.zeros((padded - rows, LANES), f32)
        for start in range(0, padded, LANES):
            block = row_part[k][start : start + LANES, :].T
            rows_buf[k][me["col"], :, start : start + LANES] = jnp.sum(
                block, axis=0, keepdims=True
            )
        cols_row_buf[k][me["row"]] = jnp.sum(col_acc[k][...], axis=0, keepdims=True)
        first = share("col", rows_buf[k], rows_sems, k)
        second = share("row", cols_row_buf[k], cr_sems, k)
        finish(second)
        cols_dp_buf[k][me["dp"]] = total_of(cols_row_buf[k], "row")
        third = share("dp", cols_dp_buf[k], cd_sems, k)
        finish(first)
        rows_next = decay_rate * row_stats[k][...] + ((1.0 - decay_rate) / (width * col_count)) * (
            total_of(rows_buf[k], "col")
        )
        out_rows[k][...] = rows_next
        inverse = lax.rsqrt(rows_next)
        for start in range(0, padded, LANES):
            row_wide[k][start : start + LANES, :] = jnp.broadcast_to(
                inverse[:, start : start + LANES], (LANES, LANES)
            ).T
        return third

    def update_pass(k, pending):
        rows, width = shapes[k]
        height = rows * dp_count * row_count
        step = block_rows(rows)
        tiles = width // LANES
        finish(pending)
        cols_next = decay_rate * col_stats[k][...] + ((1.0 - decay_rate) / height) * total_of(
            cols_dp_buf[k], "dp"
        )
        out_cols[k][...] = cols_next
        inverse = lax.rsqrt(cols_next)

        def body(i, carry):
            at = pl.ds(pl.multiple_of(i * step, step), step)
            wide = row_wide[k][at, :]
            for t in range(tiles):
                lanes = pl.ds(t * LANES, LANES)
                value = field[k][at, lanes] * wide * inverse[:, t * LANES : (t + 1) * LANES]
                field[k][at, lanes] = value
                carry = carry + fold(value * value)
            return carry

        squares = lax.fori_loop(0, rows // step, body, jnp.zeros((8, LANES), f32))
        padded = row_part[k].shape[0]
        rows_next = out_rows[k][...]
        if padded != rows:
            lane = lax.broadcasted_iota(jnp.int32, rows_next.shape, 1)
            rows_next = jnp.where(lane < rows, rows_next, 0.0)
        row_total = rows_next[:, :LANES]
        for start in range(LANES, padded, LANES):
            row_total = row_total + rows_next[:, start : start + LANES]
        row_total = jnp.broadcast_to(row_total, (8, LANES))
        sum_col_buf[k][me["col"]] = squares
        finish(share("col", sum_col_buf[k], sc_sems, k))
        sum_row_buf[k][me["row"], 0:8] = total_of(sum_col_buf[k], "col")
        sum_row_buf[k][me["row"], 8:16] = row_total
        finish(share("row", sum_row_buf[k], sr_sems, k))
        sum_dp_buf[k][me["dp"]] = total_of(sum_row_buf[k], "row")
        return share("dp", sum_dp_buf[k], sd_sems, k)

    local_out = []

    def final_pass(k, pending):
        rows, width = shapes[k]
        height = rows * dp_count * row_count
        step = block_rows(rows)
        tiles = width // LANES
        finish(pending)
        both = total_of(sum_dp_buf[k], "dp")
        squares = jnp.sum(jnp.sum(both[0:8], axis=0, keepdims=True), axis=1, keepdims=True)
        row_mean = jnp.sum(both[8:9], axis=1, keepdims=True) / height
        mean_square = row_mean * squares / (height * width * col_count)
        clip_scale = jnp.maximum(1.0, jnp.sqrt(mean_square))
        scale = jnp.broadcast_to(jnp.sqrt(row_mean) / clip_scale, (8, LANES))
        scale = jnp.broadcast_to(scale[0:1], (step, LANES))
        local_in[k][1].wait()

        def body(i, carry):
            at = pl.ds(pl.multiple_of(i * step, step), step)
            for t in range(tiles):
                lanes = pl.ds(t * LANES, LANES)
                taken = field[k][at, lanes] * scale
                updated = hold[k][at, lanes] - learn_rate * taken
                field[k][at, lanes] = taken
                hold[k][at, lanes] = updated
                weights[k][at, lanes] = updated.astype(bf16)
            return carry

        lax.fori_loop(0, rows // step, body, 0)

    def write_out(k):
        for which, (source, target) in enumerate(
            (
                (field[k], out_step[k]),
                (hold[k], out_updated[k]),
                (weights[k], out_weights[k].at[me["dp"]]),
            )
        ):
            copy = pltpu.make_async_copy(source, target, local_sems.at[6 + 3 * which + k])
            copy.start()
            local_out.append(copy)

    order = (0, 1, 2)
    first, second, third = order
    arriving = {}
    sending = []

    def launch_scatter(k, half):
        arriving[k, half] = scatter(k, half)

    def launch_gather(k, half):
        sending.extend(gather(k, half))

    def arrive(k, half):
        if half == 0:
            local_in[k][0].wait()
        finish(arriving[k, half])
        mean_pass(k, half)

    launch_scatter(first, 0)
    launch_scatter(first, 1)
    arrive(first, 0)
    launch_scatter(second, 0)
    arrive(first, 1)
    cols_first = stats(first)
    launch_scatter(second, 1)
    arrive(second, 0)
    sums_first = update_pass(first, cols_first)
    launch_scatter(third, 0)
    arrive(second, 1)
    cols_second = stats(second)
    launch_scatter(third, 1)
    final_pass(first, sums_first)
    write_out(first)
    arrive(third, 0)
    sums_second = update_pass(second, cols_second)
    launch_gather(first, 0)
    arrive(third, 1)
    cols_third = stats(third)
    launch_gather(first, 1)
    final_pass(second, sums_second)
    write_out(second)
    sums_third = update_pass(third, cols_third)
    launch_gather(second, 0)
    final_pass(third, sums_third)
    launch_gather(second, 1)
    launch_gather(third, 0)
    launch_gather(third, 1)
    write_out(third)
    finish(sending)
    for copy in local_out:
        copy.wait()


def body(axes, *args):
    dp_count, row_count, col_count = axes
    grads, masters, row_stats, col_stats = (list(args[which::4]) for which in range(4))
    shapes = tuple(master.shape for master in masters)
    grads = [g.reshape((dp_count,) + shape) for g, shape in zip(grads, shapes)]
    padded = [-(-rows // LANES) * LANES for rows, _ in shapes]
    row_stats = [
        jnp.pad(r, (0, extra - r.shape[0]), constant_values=1.0).reshape(1, extra)
        for r, extra in zip(row_stats, padded)
    ]
    col_stats = [c.reshape(1, -1) for c in col_stats]
    anywhere = pl.BlockSpec(memory_space=pl.ANY)
    inside = pl.BlockSpec(memory_space=pltpu.VMEM)
    three = range(3)

    def vmem(make, dtype=f32):
        return [pltpu.VMEM(make(k), dtype) for k in three]

    def sems(*shape):
        return [pltpu.SemaphoreType.DMA(shape)] * 2

    scratch = (
        vmem(lambda k: shapes[k], bf16)
        + vmem(lambda k: (dp_count - 1,) + shapes[k], bf16)
        + vmem(lambda k: shapes[k])
        + vmem(lambda k: shapes[k])
        + vmem(lambda k: shapes[k], bf16)
        + vmem(lambda k: (padded[k], LANES))
        + vmem(lambda k: (padded[k], LANES))
        + vmem(lambda k: (8, shapes[k][1]))
        + vmem(lambda k: (col_count, 1, padded[k]))
        + vmem(lambda k: (row_count, 1, shapes[k][1]))
        + vmem(lambda k: (dp_count, 1, shapes[k][1]))
        + vmem(lambda k: (col_count, 8, LANES))
        + vmem(lambda k: (row_count, 16, LANES))
        + vmem(lambda k: (dp_count, 16, LANES))
        + sems(3, 2, dp_count - 1)
        + sems(3, 2, dp_count - 1)
        + sems(3, col_count - 1)
        + sems(3, row_count - 1)
        + sems(3, dp_count - 1)
        + sems(3, col_count - 1)
        + sems(3, row_count - 1)
        + sems(3, dp_count - 1)
        + [pltpu.SemaphoreType.DMA((15,))]
    )
    struct = jax.ShapeDtypeStruct
    results = pl.pallas_call(
        functools.partial(kernel, axes, shapes),
        out_shape=(
            [struct(shapes[k], f32) for k in three]
            + [struct((dp_count,) + shapes[k], bf16) for k in three]
            + [struct((1, padded[k]), f32) for k in three]
            + [struct((1, shapes[k][1]), f32) for k in three]
            + [struct(shapes[k], f32) for k in three]
        ),
        in_specs=[anywhere] * 6 + [inside] * 6,
        out_specs=[anywhere] * 6 + [inside] * 6 + [anywhere] * 3,
        scratch_shapes=scratch,
        compiler_params=pltpu.CompilerParams(
            collective_id=0, has_side_effects=True, vmem_limit_bytes=60 * 1024 * 1024
        ),
    )(*grads, *masters, *row_stats, *col_stats)
    outputs = []
    for k in three:
        updated, gathered, rows_next, cols_next, taken = results[k::3]
        outputs += [
            updated,
            gathered.reshape(-1, shapes[k][1]),
            rows_next.reshape(-1)[: shapes[k][0]],
            cols_next.reshape(-1),
            taken,
        ]
    return tuple(outputs)


def solution(mesh):
    axes = tuple(mesh.shape[name] for name in ("dp", "row", "col"))
    matrix = (P("dp", "row", "col"), P(("row", "dp"), "col"), P(("row", "dp")), P("col"))
    result = (
        P(("row", "dp"), "col"),
        P("row", "col"),
        P(("row", "dp")),
        P("col"),
        P(("row", "dp"), "col"),
    )
    return jax.shard_map(
        functools.partial(body, axes),
        mesh=mesh,
        in_specs=matrix * 3,
        out_specs=result * 3,
        check_vma=False,
    )
```

time: 393 us -> 197 us (0.50); the launches traced: 387 us -> 197 us
  Pallas kernels: 0 us -> 168 us
  waiting for transfers between devices: 114 us -> 0 us
  other arithmetic: 86.1 us -> 2.59 us
  blocking collectives: 81.4 us -> 0 us
  local copies, waits for them, and re-layouts: 71.9 us -> 25.6 us
  between operations: 18.3 us -> 0.67 us
  starting transfers between devices: 15.7 us -> 0 us
    pallas_call x0 -> x1, Pallas kernels: none -> 168 us  [body(): pl.pallas_call(functools.partial(kernel, axes, shapes), out_shape=[struct...]
    all_gather x3 -> x0, waiting for transfers between devices: 102 us -> none  [finish(): lax.all_gather(updated.astype(jnp.bfloat16), 'dp', axis=0, tiled=True)]
    psum x3 -> x0, blocking collectives: 81.4 us -> none  [the longest x1 38 us: body(): lax.psum((column_parts[which], jnp.sum(rows_next)), ('dp', 'row'))]
    unnamed x3 -> x0, other arithmetic: 55 us -> none
    unnamed x51 -> x37, local copies, waits for them, and re-layouts: 62.5 us -> 23 us
    convert_element_type x3 -> x0, other arithmetic: 18.8 us -> none  [finish(): updated.astype(jnp.bfloat16)]
    all_to_all x3 -> x0, starting transfers between devices: 15.4 us -> none  [reduce_gradient(): lax.all_to_all(gradient, 'dp', split_axis=1, concat_axis=0, tiled=True)]
    reduce_sum x11 -> x0, other arithmetic: 12.3 us -> none  [the longest x3 8 us: body(): jnp.sum(update_raw * update_raw)]
  transfers between devices with their start and end apart: 6 -> 0, of which waited for: 4 -> 0; matrix products, arithmetic and copies ran while one was open for 26% -> 0% of each run, Pallas kernels for 0% -> 0%
where the time goes in v1:
time: 197 us
  Pallas kernels  168 us (85%)
  local copies, waits for them, and re-layouts  25.6 us (13%)
  other arithmetic  2.59 us (1%)
    pallas_call x1, Pallas kernels, body(): pl.pallas_call(functools.partial(kernel, axes, shapes), out_shape=[struct...  168 us
    unnamed x37, local copies, waits for them, and re-layouts  23 us

profile of v1, /device:TPU:0, one launch (start us, length us, event | category | flops | bytes accessed | tf_op | source)
XLA Modules:
  0.0 196.7 jit_solution(9484855714488003481)
XLA Ops:
  0.6 1.3 reshape.90.refs_9_
  1.9 1.3 reshape.88.refs_7_
  3.2 167.9 %shard_map.235 = (f32[512,1280]{1,0:T(8,128)}, f32[640,1024]{1,0:T(8,128)}, f32[512,1024]{1,0:T(8,128)}, bf16[2,512,1280]{2,1,0:T(8,128)(2,1)}, bf16[2,640,1024]...) custom-call(bf16[2,512,1280]{2,1,0:T(8,128)(2,1)} %bitcast.16, ...), custom_call_target="tpu_custom_call" | custom-call | tf_op jit(solution)/shard_map/pallas_call | solution.py:394
  171.1 1.3 reduce
  172.4 1.3 reduce.1
  173.7 0.0 copy-start.4
  173.7 3.6 %copy.40 = f32[512,1280]{1,0:T(8,128)} copy(f32[512,1280]{1,0:T(8,128)} %get-tuple-element.60) | data formatting | bytes 5242880
  177.2 0.0 copy-done.4
  177.2 0.0 copy-start.11
  177.3 0.0 copy-start.3
  177.3 1.5 copy.41
  178.7 0.0 copy-done.11
  178.7 0.6 copy.42
  179.3 0.6 copy-done.3
  179.9 0.0 copy-start.2
  179.9 1.5 copy.43
  181.4 1.2 copy-done.2
  182.6 0.0 copy-start.1
  182.6 1.5 copy.44
  184.1 1.2 copy-done.1
  185.3 0.0 copy-start.9
  185.3 0.0 copy-start
  185.3 1.5 copy.45
  186.8 0.0 copy-done.9
  186.8 0.6 copy.46
  187.4 0.6 copy-done
  188.0 0.0 copy-start.7
  188.0 1.5 copy.47
  189.5 1.0 copy-done.7
  190.5 0.0 copy-start.6
  190.6 1.3 copy.48
  191.9 1.0 copy-done.6
  192.9 0.0 copy-start.10
  192.9 0.0 copy-start.8
  192.9 0.0 copy-start.5
  192.9 1.3 copy.49
  194.2 0.0 copy-done.10
  194.2 0.6 copy.50
  194.8 0.0 copy-done.8
  194.8 0.6 copy.51
  195.4 0.0 copy-done.5
  195.4 1.3 copy.52
Async XLA Ops:
  173.7 3.6 %copy-start.4 = (bf16[2,512,1280]{2,1,0:T(8,128)(2,1)S(1)}, bf16[2,512,1280]{2,1,0:T(8,128)(2,1)}, u32[]{:S(2)}) copy-start(bf16[2,512,1280]{2,1,0:T(8,128)(2,1)} %get-tuple-element.31) | copy-start | bytes 7864324
  177.2 1.5 copy-start.11
  177.3 2.7 %copy-start.3 = (f32[512,1280]{1,0:T(8,128)S(1)}, f32[512,1280]{1,0:T(8,128)}, u32[]{:S(2)}) copy-start(f32[512,1280]{1,0:T(8,128)} %get-tuple-element.64) | copy-start | bytes 7864324
  179.9 2.7 %copy-start.2 = (f32[640,1024]{1,0:T(8,128)S(1)}, f32[640,1024]{1,0:T(8,128)}, u32[]{:S(2)}) copy-start(f32[640,1024]{1,0:T(8,128)} %get-tuple-element.65) | copy-start | bytes 7864324
  182.6 2.7 %copy-start.1 = (bf16[2,640,1024]{2,1,0:T(8,128)(2,1)S(1)}, bf16[2,640,1024]{2,1,0:T(8,128)(2,1)}, u32[]{:S(2)}) copy-start(bf16[2,640,1024]{2,1,0:T(8,128)(2,1)} %get-tuple-element.36) | copy-start | bytes 7864324
  185.3 1.5 copy-start.9
  185.3 2.7 %copy-start = (f32[640,1024]{1,0:T(8,128)S(1)}, f32[640,1024]{1,0:T(8,128)}, u32[]{:S(2)}) copy-start(f32[640,1024]{1,0:T(8,128)} %get-tuple-element.69) | copy-start | bytes 7864324
  188.0 2.5 %copy-start.7 = (f32[512,1024]{1,0:T(8,128)S(1)}, f32[512,1024]{1,0:T(8,128)}, u32[]{:S(2)}) copy-start(f32[512,1024]{1,0:T(8,128)} %get-tuple-element.70) | copy-start | bytes 6291460
  190.5 2.3 %copy-start.6 = (bf16[2,512,1024]{2,1,0:T(8,128)(2,1)S(1)}, bf16[2,512,1024]{2,1,0:T(8,128)(2,1)}, u32[]{:S(2)}) copy-start(bf16[2,512,1024]{2,1,0:T(8,128)(2,1)} %get-tuple-element.41) | copy-start | bytes 6291460
  192.9 1.3 copy-start.10
  192.9 1.9 copy-start.8
  192.9 2.5 %copy-start.5 = (f32[512,1024]{1,0:T(8,128)S(1)}, f32[512,1024]{1,0:T(8,128)}, u32[]{:S(2)}) copy-start(f32[512,1024]{1,0:T(8,128)} %get-tuple-element.74) | copy-start | bytes 6291460

commit v2 on v1

--- a/solution.py
+++ b/solution.py
@@ -12,6 +12,7 @@
 decay_rate = 0.9
 learn_rate = 0.01
 LANES = 128
+last = 2
 MESH = pl.DeviceIdType.MESH
 f32 = jnp.float32
 bf16 = jnp.bfloat16
@@ -199,7 +200,7 @@
         cols_dp_buf[k][me["dp"]] = total_of(cols_row_buf[k], "row")
         third = share("dp", cols_dp_buf[k], cd_sems, k)
         finish(first)
-        rows_next = decay_rate * row_stats[k][...] + ((1.0 - decay_rate) / (width * col_count)) * (
+        rows_next = decay_rate * row_stats[k][...].reshape(1, -1) + ((1.0 - decay_rate) / (width * col_count)) * (
             total_of(rows_buf[k], "col")
         )
         out_rows[k][...] = rows_next
@@ -216,7 +217,7 @@
         step = block_rows(rows)
         tiles = width // LANES
         finish(pending)
-        cols_next = decay_rate * col_stats[k][...] + ((1.0 - decay_rate) / height) * total_of(
+        cols_next = decay_rate * col_stats[k][...].reshape(1, -1) + ((1.0 - decay_rate) / height) * total_of(
             cols_dp_buf[k], "dp"
         )
         out_cols[k][...] = cols_next
@@ -285,15 +286,14 @@
             (
                 (field[k], out_step[k]),
                 (hold[k], out_updated[k]),
-                (weights[k], out_weights[k].at[me["dp"]]),
+                (weights[k], out_weights[k] if k == last else out_weights[k].at[me["dp"]]),
             )
         ):
             copy = pltpu.make_async_copy(source, target, local_sems.at[6 + 3 * which + k])
             copy.start()
             local_out.append(copy)
 
-    order = (0, 1, 2)
-    first, second, third = order
+    first, second, third = 0, 1, last
     arriving = {}
     sending = []
 
@@ -336,11 +336,31 @@
     launch_gather(second, 0)
     final_pass(third, sums_third)
     launch_gather(second, 1)
-    launch_gather(third, 0)
-    launch_gather(third, 1)
     write_out(third)
     finish(sending)
     for copy in local_out:
+        copy.wait()
+
+
+def write_results(*refs):
+    small_in, large_in = refs[0:6], refs[6:15]
+    small_out, large_out = refs[15:21], list(refs[21:30])
+    held, (in_sems, out_sems) = refs[30:39], refs[39:41]
+    large_out[3 + last] = large_out[3 + last].at[lax.axis_index("dp")]
+    reads = [
+        pltpu.make_async_copy(large_in[i], held[i], in_sems.at[i]) for i in range(len(held))
+    ]
+    writes = [
+        pltpu.make_async_copy(held[i], large_out[i], out_sems.at[i]) for i in range(len(held))
+    ]
+    for copy in reads:
+        copy.start()
+    for source, target in zip(small_in, small_out):
+        target[...] = source[0, :]
+    for read, write in zip(reads, writes):
+        read.wait()
+        write.start()
+    for copy in writes:
         copy.wait()
 
 
@@ -351,10 +371,9 @@
     grads = [g.reshape((dp_count,) + shape) for g, shape in zip(grads, shapes)]
     padded = [-(-rows // LANES) * LANES for rows, _ in shapes]
     row_stats = [
-        jnp.pad(r, (0, extra - r.shape[0]), constant_values=1.0).reshape(1, extra)
+        jnp.pad(r, (0, extra - r.shape[0]), constant_values=1.0)
         for r, extra in zip(row_stats, padded)
     ]
-    col_stats = [c.reshape(1, -1) for c in col_stats]
     anywhere = pl.BlockSpec(memory_space=pl.ANY)
     inside = pl.BlockSpec(memory_space=pltpu.VMEM)
     three = range(3)
@@ -395,7 +414,7 @@
         functools.partial(kernel, axes, shapes),
         out_shape=(
             [struct(shapes[k], f32) for k in three]
-            + [struct((dp_count,) + shapes[k], bf16) for k in three]
+            + [struct(shapes[k] if k == last else (dp_count,) + shapes[k], bf16) for k in three]
             + [struct((1, padded[k]), f32) for k in three]
             + [struct((1, shapes[k][1]), f32) for k in three]
             + [struct(shapes[k], f32) for k in three]
@@ -407,15 +426,47 @@
             collective_id=0, has_side_effects=True, vmem_limit_bytes=60 * 1024 * 1024
         ),
     )(*grads, *masters, *row_stats, *col_stats)
+    smalls = list(results[6:12])
+    larges = list(results[0:6]) + list(results[12:15])
+    mine = results[3 + last]
+    received = [
+        lax.ppermute(
+            mine, "dp", [(source, (source + offset) % dp_count) for source in range(dp_count)]
+        )
+        for offset in range(1, dp_count)
+    ]
+    moved = 2 * sum(large.size * large.dtype.itemsize for large in larges)
+    written = pl.pallas_call(
+        write_results,
+        out_shape=(
+            [struct(small.shape[1:], f32) for small in smalls]
+            + [
+                struct((dp_count,) + large.shape if which == 3 + last else large.shape, large.dtype)
+                for which, large in enumerate(larges)
+            ]
+        ),
+        in_specs=[inside] * 6 + [anywhere] * 9,
+        out_specs=[inside] * 6 + [anywhere] * 9,
+        scratch_shapes=[pltpu.VMEM(large.shape, large.dtype) for large in larges]
+        + [pltpu.SemaphoreType.DMA((9,))] * 2,
+        compiler_params=pltpu.CompilerParams(vmem_limit_bytes=60 * 1024 * 1024),
+        cost_estimate=pl.CostEstimate(flops=0, bytes_accessed=moved, transcendentals=0),
+    )(*smalls, *larges)
+    gathered = list(written[9:12])
+    me = lax.axis_index("dp")
+    for offset in range(1, dp_count):
+        source = lax.rem(me + dp_count - offset, dp_count)
+        gathered[last] = lax.dynamic_update_index_in_dim(
+            gathered[last], received[offset - 1], source, 0
+        )
     outputs = []
     for k in three:
-        updated, gathered, rows_next, cols_next, taken = results[k::3]
         outputs += [
-            updated,
-            gathered.reshape(-1, shapes[k][1]),
-            rows_next.reshape(-1)[: shapes[k][0]],
-            cols_next.reshape(-1),
-            taken,
+            written[6 + k],
+            gathered[k].reshape(-1, shapes[k][1]),
+            written[k][: shapes[k][0]],
+            written[3 + k],
+            written[12 + k],
         ]
     return tuple(outputs)
 

time: 197 us -> 172 us (0.87)
  local copies, waits for them, and re-layouts: 25.6 us -> 1.04 us
  waiting for transfers between devices: 0 us -> 7.42 us
  Pallas kernels: 168 us -> 162 us
  other arithmetic: 2.59 us -> 0 us
    unnamed x37 -> x0, local copies, waits for them, and re-layouts: 23 us -> none
    pallas_call x1, Pallas kernels: 168 us -> 145 us  [body(): pl.pallas_call(functools.partial(kernel, axes, shapes), out_shape=[struct...]
    pallas_call x0 -> x1, Pallas kernels: none -> 16.3 us  [body(): pl.pallas_call(write_results, out_shape=[struct(small.shape[1:], f32) for...]
    ppermute x0 -> x1, waiting for transfers between devices: none -> 7.42 us  [body(): lax.ppermute(mine, 'dp', [(source, (source + offset) % dp_count) for sour...]
    pallas_call x2 -> x0, other arithmetic: 2.59 us -> none  [body(): pl.pallas_call(functools.partial(kernel, axes, shapes), out_shape=[struct...]
    reshape x2 -> x0, local copies, waits for them, and re-layouts: 2.56 us -> none  [the longest x1 1.29 us: body(): col_stats = [c.reshape(1, -1) for c in col_stats]]
  transfers between devices with their start and end apart: 0 -> 1, of which waited for: 0 -> 1; matrix products, arithmetic and copies ran while one was open for 0% -> 0% of each run, Pallas kernels for 0% -> 9%
where the time goes in v2:
time: 172 us; the launch traced here: 171 us
  Pallas kernels  162 us (94%)
  waiting for transfers between devices  7.42 us (4%)
    pallas_call x1, Pallas kernels, body(): pl.pallas_call(functools.partial(kernel, axes, shapes), out_shape=[struct...  145 us
    pallas_call x1, Pallas kernels, body(): pl.pallas_call(write_results, out_shape=[struct(small.shape[1:], f32) for...  16.3 us
    ppermute x1, waiting for transfers between devices, body(): lax.ppermute(mine, 'dp', [(source, (source + offset) % dp_count) for sour...  7.42 us
  transfers between devices with their start and end apart: 1, of which 1 were waited for; matrix products, arithmetic and copies ran while one was open for 0% of the time, Pallas kernels for 9%

profile of v2, /device:TPU:0, one launch (start us, length us, event | category | flops | bytes accessed | tf_op | source)
XLA Modules:
  0.0 171.5 jit_solution(6492855800733339580)
XLA Ops:
  0.7 145.5 %shard_map.235 = (f32[512,1280]{1,0:T(8,128)}, f32[640,1024]{1,0:T(8,128)}, f32[512,1024]{1,0:T(8,128)}, bf16[2,512,1280]{2,1,0:T(8,128)(2,1)}, bf16[2,640,1024]...) custom-call(bf16[2,512,1280]{2,1,0:T(8,128)(2,1)} %bitcast.8, ...), custom_call_target="tpu_custom_call" | custom-call | tf_op jit(solution)/shard_map/pallas_call | solution.py:413
  146.1 0.6 collective-permute-start
  146.7 16.3 %shard_map.236 = (f32[512]{0:T(512)}, f32[640]{0:T(1024)}, f32[512]{0:T(512)}, f32[1280]{0:T(1024)}, f32[1024]{0:T(1024)}, /*index=5*/f32[1024]{0:T(1024)}, f32[...) custom-call(f32[1,512]{1,0:T(1,128)} %get-tuple-element.45.refs_0_, ...), custom_call_target="tpu_custom_call" | custom-call | bytes 41943040 | tf_op jit(solution)/shard_map/pallas_call | solution.py:439
  163.0 7.4 %collective-permute-done = bf16[512,1024]{1,0:T(8,128)(2,1)S(1)} collective-permute-done((bf16[512,1024]{1,0:T(8,128)(2,1)}, bf16[512,1024]{1,0:T(8,128)(2,1)S(1)}, u32[]{:S(2)}, u32[]{:S(2)}) %collective-permute-start) | collective-permute-done | bytes 1048608 | tf_op jit(solution)/shard_map/ppermute | solution.py:433
  170.4 1.0 bitcast_dynamic-update-slice_fusion
Async XLA Ops:
  146.1 24.3 %collective-permute-start = (bf16[512,1024]{1,0:T(8,128)(2,1)}, bf16[512,1024]{1,0:T(8,128)(2,1)S(1)}, u32[]{:S(2)}, u32[]{:S(2)}) collective-permute-start(bf16[512,1024]{1,0:T(8,128)(2,1)} %get-tuple-element.56.refs_11_), channel_id=1, source_target_pairs={{0,16},{16,0},{1,17},{17,1},{2,18},{18,2},{3,19},{19,3},{4,20},{20... | collective-permute-start | bytes 3145736 | tf_op jit(solution)/shard_map/ppermute | solution.py:433

commit v3 on v2

--- a/solution.py
+++ b/solution.py
@@ -98,7 +98,7 @@
         return copies
 
     def gather(k, half):
-        part = rows_of(k, half)
+        part = pl.ds(0, shapes[k][0]) if half is None else rows_of(k, half)
         copies = []
         if part is not None:
             for offset in range(1, dp_count):
@@ -106,8 +106,8 @@
                     pltpu.make_async_remote_copy(
                         src_ref=weights[k].at[part],
                         dst_ref=out_weights[k].at[me["dp"], part],
-                        send_sem=ag_sems[0].at[k, half, offset - 1],
-                        recv_sem=ag_sems[1].at[k, half, offset - 1],
+                        send_sem=ag_sems[0].at[k, half or 0, offset - 1],
+                        recv_sem=ag_sems[1].at[k, half or 0, offset - 1],
                         device_id={"dp": peer("dp", offset)},
                         device_id_type=MESH,
                     )
@@ -333,9 +333,8 @@
     final_pass(second, sums_second)
     write_out(second)
     sums_third = update_pass(third, cols_third)
-    launch_gather(second, 0)
+    launch_gather(second, None)
     final_pass(third, sums_third)
-    launch_gather(second, 1)
     write_out(third)
     finish(sending)
     for copy in local_out:

time: 172 us -> 172 us (level)
  no operation moved by 1% of the time
where the time goes in v3:
time: 172 us; the launch traced here: 171 us
  Pallas kernels  162 us (94%)
  waiting for transfers between devices  7.42 us (4%)
    pallas_call x1, Pallas kernels, body(): pl.pallas_call(functools.partial(kernel, axes, shapes), out_shape=[struct...  145 us
    pallas_call x1, Pallas kernels, body(): pl.pallas_call(write_results, out_shape=[struct(small.shape[1:], f32) for...  16.3 us
    ppermute x1, waiting for transfers between devices, body(): lax.ppermute(mine, 'dp', [(source, (source + offset) % dp_count) for sour...  7.42 us
  transfers between devices with their start and end apart: 1, of which 1 were waited for; matrix products, arithmetic and copies ran while one was open for 0% of the time, Pallas kernels for 9%

profile of v3, /device:TPU:0, one launch (start us, length us, event | category | flops | bytes accessed | tf_op | source)
XLA Modules:
  0.0 171.5 jit_solution(18251521754575360940)
XLA Ops:
  0.7 145.5 %shard_map.235 = (f32[512,1280]{1,0:T(8,128)}, f32[640,1024]{1,0:T(8,128)}, f32[512,1024]{1,0:T(8,128)}, bf16[2,512,1280]{2,1,0:T(8,128)(2,1)}, bf16[2,640,1024]...) custom-call(bf16[2,512,1280]{2,1,0:T(8,128)(2,1)} %bitcast.8, ...), custom_call_target="tpu_custom_call" | custom-call | tf_op jit(solution)/shard_map/pallas_call | solution.py:412
  146.1 0.6 collective-permute-start
  146.7 16.3 %shard_map.236 = (f32[512]{0:T(512)}, f32[640]{0:T(1024)}, f32[512]{0:T(512)}, f32[1280]{0:T(1024)}, f32[1024]{0:T(1024)}, /*index=5*/f32[1024]{0:T(1024)}, f32[...) custom-call(f32[1,512]{1,0:T(1,128)} %get-tuple-element.45.refs_0_, ...), custom_call_target="tpu_custom_call" | custom-call | bytes 41943040 | tf_op jit(solution)/shard_map/pallas_call | solution.py:438
  163.0 7.4 %collective-permute-done = bf16[512,1024]{1,0:T(8,128)(2,1)S(1)} collective-permute-done((bf16[512,1024]{1,0:T(8,128)(2,1)}, bf16[512,1024]{1,0:T(8,128)(2,1)S(1)}, u32[]{:S(2)}, u32[]{:S(2)}) %collective-permute-start) | collective-permute-done | bytes 1048608 | tf_op jit(solution)/shard_map/ppermute | solution.py:432
  170.4 1.0 bitcast_dynamic-update-slice_fusion
Async XLA Ops:
  146.1 24.3 %collective-permute-start = (bf16[512,1024]{1,0:T(8,128)(2,1)}, bf16[512,1024]{1,0:T(8,128)(2,1)S(1)}, u32[]{:S(2)}, u32[]{:S(2)}) collective-permute-start(bf16[512,1024]{1,0:T(8,128)(2,1)} %get-tuple-element.56.refs_11_), channel_id=1, source_target_pairs={{0,16},{16,0},{1,17},{17,1},{2,18},{18,2},{3,19},{19,3},{4,20},{20... | collective-permute-start | bytes 3145736 | tf_op jit(solution)/shard_map/ppermute | solution.py:432
